TPU v7x, 32 devices: a whole 2x2x4 slice. The times are simulated.
32 devices in a mesh: tok: 16 (over z, y, x), exp: 2 (over core).
Axes of the slice: x: 2, y: 2, z: 4, core: 2. Of those that a mesh axis runs over, the one named last changes fastest.
Arguments:
- activations: bfloat16 [384, 14336], P(('tok', 'exp')), may hold values from -6 to 6
- expert_ids: int32 [384, 2], P(('tok', 'exp')), may hold values from 0 to 7, all different within a row; in each aligned block of 12 rows (0 to 11, 12 to 23, ...) at most 4 rows name the same one
Outputs:
- hessian: float32 [2, 14336, 14336], P('exp', 'tok')
Inputs may be any that keep to these rules, and one draw needn't show every extreme that they name: `expert_ids`: each row names 2 different experts. Among the 12 rows of one device no expert is named more than 4 times, some expert exactly 4 times; every expert is named by some row.
All inputs are finite; a program needn't handle non-finite values.
Results may differ from a plain program's by a relative error of at most 0.0003.
Values may be sent and summed in bfloat16 or wider, within the bound.
No kernel may reach another device: no remote copies, remote signals or barrier semaphores. Data moves between devices by JAX's collectives and lax.ppermute only.
A program may use at most 128 MiB of HBM per device.

v0:
```python
import jax
import jax.numpy as jnp
from jax import lax
from jax.sharding import PartitionSpec as P

CAP = 4


def place_tokens(activations, expert_ids, window_size):
    expert_labels = jnp.arange(window_size, dtype=jnp.int32)
    routed = jnp.any(expert_ids[:, :, None] == expert_labels[None, None, :], axis=1).astype(
        jnp.int32
    )
    ranking = jnp.cumsum(routed, axis=0) - 1
    slot_labels = jnp.arange(CAP, dtype=jnp.int32)
    placement = (routed.T[:, None, :] == 1) & (ranking.T[:, None, :] == slot_labels[None, :, None])
    placement_b = placement.astype(jnp.bfloat16)
    send_slots = jnp.einsum(
        "gct,tf->gcf", placement_b, activations, preferred_element_type=jnp.float32
    ).astype(jnp.bfloat16)
    send_marks = jnp.sum(placement.astype(jnp.float32), axis=2).astype(jnp.bfloat16)
    return (send_slots, send_marks)


def shards(activations, expert_ids):
    window_size = lax.axis_size("exp")
    send_slots, send_marks = place_tokens(activations, expert_ids, window_size)
    owned, present = (
        lax.all_to_all(send_slots, "exp", split_axis=0, concat_axis=1, tiled=True),
        lax.all_to_all(send_marks, "exp", split_axis=0, concat_axis=1, tiled=True),
    )
    feature_width = activations.shape[1]
    group_size = lax.axis_size("tok")
    row_count = feature_width // group_size
    row_start = lax.axis_index("tok") * row_count
    gathered, marks = (
        lax.all_gather(owned, "tok", axis=1, tiled=True),
        lax.all_gather(present, "tok", axis=1, tiled=True),
    )
    all_tokens = gathered[0]
    chosen = lax.dynamic_slice_in_dim(all_tokens, row_start, row_count, 1)
    product = lax.dot_general(
        chosen, all_tokens, (((0,), (0,)), ((), ())), preferred_element_type=jnp.float32
    )
    routed_total = jnp.sum(marks.astype(jnp.float32))
    return (product * (2.0 / routed_total))[None]


def solution(mesh):
    in_specs = (P(("tok", "exp"), None), P(("tok", "exp"), None))
    out_specs = P("exp", "tok", None)
    return jax.shard_map(shards, mesh=mesh, in_specs=in_specs, out_specs=out_specs, check_vma=False)
```

profile of v0, /device:TPU:0, one launch (start us, length us, event | category | flops | bytes accessed | tf_op | source)
XLA Modules:
  0.0 116.5 jit_solution(18362874523706911534)
XLA Ops:
  6.5 0.0 copy-start
  6.5 0.0 all-gather.2.cloned.1.call-start
  6.5 0.7 compare_reduce_fusion
  7.3 0.2 reduce_window_sum.11
  7.5 0.1 copy-done
  7.6 0.2 convolution_convert_fusion
  7.8 3.9 %all_to_all.25 = bf16[2,4,14336]{2,1,0:T(4,128)(2,1)S(1)} all-to-all(bf16[2,4,14336]{2,1,0:T(4,128)(2,1)S(1)} %convolution_convert_fusion), channel_id=1, replica_groups=mesh['tok'=16,'exp'=2] {'exp'}, dimensions={0} | all-to-all | bytes 458752 | tf_op jit(solution)/shard_map/all_to_all | solution.py:29
  11.7 0.7 all_to_all.20
  12.4 0.0 all-gather.2.cloned.1.call-update
  12.5 0.1 convert_reduce_fusion
  12.5 0.6 copy.8
  13.1 3.1 %all-to-all-start.1 = ((bf16[2,1,4]{2,1,0:T(2,128)(2,1)}), bf16[2,1,4]{2,1,0:T(2,128)(2,1)S(1)}, u32[]{:S(2)}, u32[]{:S(2)}) async-start(bf16[2,1,4]{2,1,0:T(2,128)(2,1)} %copy.8), calls=%async_computation.1 | async-start | bytes 2048 | tf_op jit(solution)/shard_map/all_to_all | solution.py:30
  16.3 1.3 %all-to-all-done.1 = bf16[2,1,4]{2,1,0:T(2,128)(2,1)S(1)} async-done(((bf16[2,1,4]{2,1,0:T(2,128)(2,1)}), bf16[2,1,4]{2,1,0:T(2,128)(2,1)S(1)}, u32[]{:S(2)}, u32[]{:S(2)}) %all-to-all-start.1) | async-done | bytes 48 | tf_op jit(solution)/shard_map/all_to_all | solution.py:30
  17.7 0.1 reshape.22
  17.8 1.2 %dynamic-slice.1 = u32[1]{0:T(128)} dynamic-slice(u32[32]{0:T(128)} %constant.31, u32[]{:T(128)S(6)} %add.7), dynamic_slice_sizes={1} | dynamic-slice | bytes 12
  19.6 0.2 dynamic-update-slice
  19.8 43.9 %all-reduce = bf16[128]{0:T(256)(128)(2,1)S(1)} all-reduce(bf16[128]{0:T(256)(128)(2,1)S(1)} %dynamic-update-slice), channel_id=1, replica_groups=mesh['tok'=16,'exp'=2] {'tok'}, use_global_device_ids=true, to_apply=%add | all-reduce | flops 128 | bytes 512
  63.7 0.6 convert_reduce_fusion.1
  64.9 22.2 %all-gather.2.cloned.1.call-done = bf16[1,128,14336]{2,1,0:T(8,128)(2,1)} async-done(((bf16[1,8,14336]{2,1,0:T(8,128)(2,1)}), bf16[1,128,14336]{2,1,0:T(8,128)(2,1)}) %all-gather.2.cloned.1.call-update) | async-done | bytes 3670032 | tf_op jit(solution)/shard_map/all_gather | solution.py:37
  87.1 22.6 %multiply_bitcast_fusion = f32[1,896,14336]{2,1,0:T(8,128)} fusion(f32[]{:T(128)S(6)} %div.3, bf16[1,128,14336]{2,1,0:T(8,128)(2,1)} %all-gather.2.cloned.1.call-done, s32[]{:T(128)S(6)} %select_n.3), kind=kOutput, calls=%fused_computation | convolution fusion | flops 3301179392 | bytes 55279624 | tf_op jit(solution)/shard_map/dot_general | solution.py:42
  (4 shorter events, 0.0 us)
Async XLA Ops:
  6.5 1.0 copy-start
  6.5 80.6 %all-gather.2.cloned.1.call-start = ((), (), s32[]{:S(2)}) async-start(), calls=%async_computation.2 | async-start | bytes 3899392 | tf_op jit(solution)/shard_map/all_gather | solution.py:37
  13.1 4.5 %all-to-all-start.1 = ((bf16[2,1,4]{2,1,0:T(2,128)(2,1)}), bf16[2,1,4]{2,1,0:T(2,128)(2,1)S(1)}, u32[]{:S(2)}, u32[]{:S(2)}) async-start(bf16[2,1,4]{2,1,0:T(2,128)(2,1)} %copy.8), calls=%async_computation.1 | async-start | bytes 2048 | tf_op jit(solution)/shard_map/all_to_all | solution.py:30
Sparse Core Ops, SparseCore 0:
  12.6 74.5 all-gather.1
where the time goes:
time: 117 us
  blocking collectives  47.8 us (41%)
  waiting for transfers between devices  23.6 us (20%)
  matrix products  22.8 us (19%)
  between operations  14.6 us (12%)
  starting transfers between devices  3.14 us (3%)
  local copies, waits for them, and re-layouts  2.99 us (3%)
  other arithmetic  1.66 us (1%)
    unnamed x1, blocking collectives  43.9 us
    dot_general x1, matrix products, shards(): lax.dot_general(chosen, all_tokens, (((0,), (0,)), ((), ())), preferred_e...  22.6 us
    all_gather x1, waiting for transfers between devices, shards(): lax.all_gather(owned, 'tok', axis=1, tiled=True)  22.2 us
    all_to_all x1, blocking collectives, shards(): lax.all_to_all(send_slots, 'exp', split_axis=0, concat_axis=1, tiled=True)  3.9 us
    all_to_all x1, starting transfers between devices, shards(): lax.all_to_all(send_marks, 'exp', split_axis=0, concat_axis=1, tiled=True)  3.14 us
  transfers between devices with their start and end apart: 2, of which 2 were waited for; matrix products, arithmetic and copies ran while one was open for 2% of the time, Pallas kernels for 0%

commit v1 on v0

v1 whole, which is shorter than its diff:
```python
import functools

import jax
import jax.numpy as jnp
from jax import lax
from jax.experimental import pallas as pl
from jax.experimental.pallas import tpu as pltpu
from jax.sharding import PartitionSpec as P

CAP = 4
LANES = 128
F32 = jnp.float32
BF16 = jnp.bfloat16


def tok_dims(mesh):
    n = mesh.shape["tok"]
    try:
        line = [tuple(d.coords) for d in mesh.devices.reshape(n, -1)[:, 0]]
        found = []
        for axis in range(3):
            size = len({c[axis] for c in line})
            if size > 1:
                stride = next(t for t in range(n) if line[t][axis] != line[0][axis])
                found.append((stride, size))
        sizes = [size for _, size in sorted(found, reverse=True)]
    except AttributeError:
        sizes = []
        while n > 1:
            part = 2 if n % 2 == 0 and len(sizes) < 2 else n
            sizes.append(part)
            n //= part
        sizes = sizes[::-1]
    while len(sizes) > 3:
        sizes = [sizes[0] * sizes[1]] + sizes[2:]
    return tuple(sizes + [1] * (3 - len(sizes)))


def slots_kernel(where, ids, act, out, *, experts, blocks, chunk):
    me, z = where[0], where[1]
    rows = act.shape[0]
    earlier = (
        lax.broadcasted_iota(jnp.int32, (rows, rows), 1) < lax.broadcasted_iota(jnp.int32, (rows, rows), 0)
    ).astype(F32)
    slot = lax.broadcasted_iota(jnp.int32, (rows, LANES), 1)
    for j in range(experts):
        expert = lax.rem(me + j, experts)
        hit = jnp.max((ids[...] == expert).astype(F32), axis=1, keepdims=True)
        wide = jnp.broadcast_to(hit, (rows, LANES))
        rank = jnp.dot(earlier, wide, preferred_element_type=F32)
        place = jnp.where((wide > 0.5) & (rank.astype(jnp.int32) == slot), 1.0, 0.0)
        place = place.T[:CAP].astype(BF16)
        for b in range(blocks):
            source = pl.multiple_of(comb(z, b, blocks) * chunk, LANES)
            out[j, :, b * chunk : (b + 1) * chunk] = jnp.dot(
                place, act[:, pl.ds(source, chunk)], preferred_element_type=F32
            ).astype(BF16)
        out[j, :, blocks * chunk :] = jnp.broadcast_to(
            jnp.sum(place.astype(F32), axis=1, keepdims=True), (CAP, LANES)
        ).astype(BF16)


def comb(a, b, n):
    return a ^ b if n & (n - 1) == 0 else (a + b) % n


def uncomb(k, d, n):
    return k ^ d if n & (n - 1) == 0 else (k + d) % n


def gram_kernel(where, *refs, pieces, rows, columns, tile, aliased):
    refs = refs[1:] if aliased else refs
    left, scale = refs[:2]
    parts = refs[2 : 2 + pieces]
    out = refs[2 + pieces]
    right, held, sems = refs[3 + pieces :]
    at = 0
    for part in parts:
        n = part.shape[0]
        right[at : at + n, :] = part[:, :columns]
        at += n
    factor = scale[0:1, 0:1]
    start = pl.multiple_of(where[0] * columns, LANES)
    copies = []
    for i in range(rows // tile):
        held[i] = (
            lax.dot_general(
                left[i * tile : (i + 1) * tile, :], right[...], (((1,), (0,)), ((), ())), preferred_element_type=F32
            )
            * factor
        )
        copies.append(
            pltpu.make_async_copy(
                held.at[i], out.at[0, pl.ds(i * tile, tile), pl.ds(start, columns)], sems.at[i]
            )
        )
        copies[-1].start()
    for copy in copies:
        copy.wait()


def gram(where, left, scale, parts, before, columns, width):
    rows, tokens = left.shape
    tile = next(t for t in (128, 112, 64, 56, 32, 16, 8, rows) if rows % t == 0)
    n = len(parts)
    specs = [pl.BlockSpec(memory_space=pltpu.VMEM)] * (2 + n)
    args = [left, scale, *parts]
    if before is not None:
        specs, args = [pl.BlockSpec(memory_space=pl.ANY)] + specs, [before] + args
    return pl.pallas_call(
        functools.partial(
            gram_kernel, pieces=n, rows=rows, columns=columns, tile=tile, aliased=before is not None
        ),
        grid_spec=pltpu.PrefetchScalarGridSpec(
            num_scalar_prefetch=1,
            grid=(),
            in_specs=specs,
            out_specs=pl.BlockSpec(memory_space=pl.ANY),
            scratch_shapes=[
                pltpu.VMEM((tokens, columns), BF16),
                pltpu.VMEM((rows // tile, tile, columns), F32),
                pltpu.SemaphoreType.DMA((rows // tile,)),
            ],
        ),
        out_shape=jax.ShapeDtypeStruct((1, rows, width), F32),
        input_output_aliases={} if before is None else {1: 0},
        compiler_params=pltpu.CompilerParams(vmem_limit_bytes=30 * 2**20),
        cost_estimate=pl.CostEstimate(
            flops=2 * rows * tokens * columns, bytes_accessed=4 * rows * columns, transcendentals=0
        ),
        name="gram",
    )(where, *args)


def left_kernel(where, *refs, rows, columns):
    parts, (left, scale) = refs[:-2], refs[-2:]
    start = pl.multiple_of(where[0] * rows, LANES)
    chosen = jnp.concatenate([part[:, pl.ds(start, rows)].astype(F32) for part in parts], axis=0)
    left[...] = chosen.T.astype(BF16)
    count = sum(jnp.sum(part[:, columns:].astype(F32), axis=0, keepdims=True) for part in parts)
    scale[...] = jnp.broadcast_to(2.0 / count, scale.shape)


def left_operand(where, parts, rows, columns):
    tokens = sum(part.shape[0] for part in parts)
    if rows % LANES:
        whole = jnp.concatenate(parts, axis=0)
        chosen = lax.dynamic_slice_in_dim(whole, where[0] * rows, rows, 1)
        count = jnp.sum(whole[:, columns].astype(F32))
        return chosen.T, jnp.full((8, LANES), 2.0 / count, F32)
    return pl.pallas_call(
        functools.partial(left_kernel, rows=rows, columns=columns),
        grid_spec=pltpu.PrefetchScalarGridSpec(
            num_scalar_prefetch=1,
            grid=(),
            in_specs=[pl.BlockSpec(memory_space=pltpu.VMEM)] * len(parts),
            out_specs=[pl.BlockSpec(memory_space=pltpu.VMEM)] * 2,
        ),
        out_shape=[jax.ShapeDtypeStruct((rows, tokens), BF16), jax.ShapeDtypeStruct((8, LANES), F32)],
        cost_estimate=pl.CostEstimate(flops=rows * tokens * 64, bytes_accessed=4 * rows * tokens, transcendentals=0),
        name="left",
    )(where, *parts)


def solution(mesh):
    dims = tok_dims(mesh)
    experts = mesh.shape["exp"]
    n0, n1, n2 = dims
    group = n0 * n1 * n2

    def index(c):
        return (c[0] * n1 + c[1]) * n2 + c[2]

    coords = [(a, b, c) for a in range(n0) for b in range(n1) for c in range(n2)]

    def hops(axis_of, d):
        pairs = []
        for c in coords:
            for e in range(experts):
                axis = axis_of(e)
                to = list(c)
                to[axis] = comb(c[axis], d, dims[axis])
                pairs.append((index(c) * experts + e, index(to) * experts + e))
        return pairs

    def send(value, axis_of, d):
        return lax.ppermute(value, ("tok", "exp"), hops(axis_of, d))

    mirrored = n1 == n2
    first = lambda e: 1 + (e + 1) % 2 if mirrored else 2
    second = lambda e: 3 - first(e)

    def shards(activations, expert_ids):
        rows_in, width = activations.shape
        rows = width // group
        chunk = width // n0
        tok, exp = lax.axis_index("tok"), lax.axis_index("exp")
        z = tok // (n1 * n2)
        where = jnp.stack([exp, z]).astype(jnp.int32)
        slots = pl.pallas_call(
            functools.partial(slots_kernel, experts=experts, blocks=n0, chunk=chunk),
            grid_spec=pltpu.PrefetchScalarGridSpec(
                num_scalar_prefetch=1,
                grid=(),
                in_specs=[pl.BlockSpec(memory_space=pltpu.VMEM)] * 2,
                out_specs=pl.BlockSpec(memory_space=pltpu.VMEM),
            ),
            out_shape=jax.ShapeDtypeStruct((experts, CAP, width + LANES), BF16),
            name="slots",
        )(where, expert_ids, activations)
        mine = [slots[0]]
        for j in range(1, experts):
            mine.append(lax.ppermute(slots[j], "exp", [(e, (e + j) % experts) for e in range(experts)]))
        marks = jnp.concatenate([m[:, width:] for m in mine], axis=0)

        def block(b, marked):
            value = jnp.concatenate([m[:, b * chunk : (b + 1) * chunk] for m in mine], axis=0)
            return jnp.concatenate([value, marks], axis=1) if marked else value

        place = (tok % (n1 * n2)).astype(jnp.int32)[None]
        out = left = scale = None
        for k in range(n0):
            line = [block(k, k == 0)]
            for d in range(1, n0):
                line.append(send(block(uncomb(k, d, n0), k == 0), lambda e: 0, d))
            half = jnp.concatenate(line, axis=0)
            plane = [half] + [send(half, first, d) for d in range(1, dims[first(0)])]
            half = jnp.concatenate(plane, axis=0)
            parts = [half] + [send(half, second, d) for d in range(1, dims[second(0)])]
            if k == 0:
                left, scale = left_operand(place, parts, rows, chunk)
            at = comb(z, k, n0).astype(jnp.int32)[None]
            out = gram(at, left, scale, parts, out, chunk, width)
        return out

    in_specs = (P(("tok", "exp"), None), P(("tok", "exp"), None))
    return jax.shard_map(shards, mesh=mesh, in_specs=in_specs, out_specs=P("exp", "tok", None), check_vma=False)
```

time: 117 us -> 97 us (0.83)
  blocking collectives: 47.8 us -> 0 us
  Pallas kernels: 0 us -> 26.8 us
  matrix products: 22.8 us -> 0 us
  starting transfers between devices: 3.14 us -> 25.7 us
  between operations: 14.6 us -> 0.18 us
  local copies, waits for them, and re-layouts: 2.99 us -> 13.4 us
  waiting for transfers between devices: 23.6 us -> 29.4 us
    unnamed x1 -> x0, blocking collectives: 43.9 us -> none
    ppermute x0 -> x21, waiting for transfers between devices: none -> 29.4 us  [the longest x20 28.5 us: send(): return lax.ppermute(value, ('tok', 'exp'), hops(axis_of, d))]
    pallas_call x0 -> x6, Pallas kernels: none -> 26.8 us  [the longest x4 21.6 us: gram(): pl.pallas_call(functools.partial(gram_kernel, pieces=n, rows=rows, column...]
    ppermute x0 -> x21, starting transfers between devices: none -> 25.7 us  [the longest x20 25.2 us: send(): return lax.ppermute(value, ('tok', 'exp'), hops(axis_of, d))]
    dot_general x2 -> x0, matrix products: 22.8 us -> none  [the longest x1 22.6 us: shards(): lax.dot_general(chosen, all_tokens, (((0,), (0,)), ((), ())), preferred_e...]
    all_gather x1 -> x0, waiting for transfers between devices: 22.2 us -> none  [shards(): lax.all_gather(owned, 'tok', axis=1, tiled=True)]
    concatenate x0 -> x7, local copies, waits for them, and re-layouts: none -> 6.47 us  [the longest x3 5.13 us: shards(): half = jnp.concatenate(line, axis=0)]
    unnamed x6 -> x18, local copies, waits for them, and re-layouts: 1.65 us -> 5.85 us
  transfers between devices with their start and end apart: 2 -> 21, of which waited for: 2 -> 8; matrix products, arithmetic and copies ran while one was open for 2% -> 7% of each run, Pallas kernels for 0% -> 18%
where the time goes in v1:
time: 97 us; the launch traced here: 96.5 us
  waiting for transfers between devices  29.4 us (30%)
  Pallas kernels  26.8 us (28%)
  starting transfers between devices  25.7 us (26%)
  local copies, waits for them, and re-layouts  13.4 us (14%)
    ppermute x20, waiting for transfers between devices, send(): return lax.ppermute(value, ('tok', 'exp'), hops(axis_of, d))  28.5 us
    ppermute x20, starting transfers between devices, send(): return lax.ppermute(value, ('tok', 'exp'), hops(axis_of, d))  25.2 us
    pallas_call x4, Pallas kernels, gram(): pl.pallas_call(functools.partial(gram_kernel, pieces=n, rows=rows, column...  21.6 us
    unnamed x18, local copies, waits for them, and re-layouts  5.85 us
    concatenate x3, local copies, waits for them, and re-layouts, shards(): half = jnp.concatenate(line, axis=0)  5.13 us
    pallas_call x1, Pallas kernels, shards(): pl.pallas_call(functools.partial(slots_kernel, experts=experts, blocks=n0...  3.24 us
    pallas_call x1, Pallas kernels, left_operand(): pl.pallas_call(functools.partial(left_kernel, rows=rows, columns=columns)...  1.98 us
  transfers between devices with their start and end apart: 21, of which 8 were waited for; matrix products, arithmetic and copies ran while one was open for 7% of the time, Pallas kernels for 18%

profile of v1, /device:TPU:0, one launch (start us, length us, event | category | flops | bytes accessed | tf_op | source)
XLA Modules:
  0.0 96.5 jit_solution(8658695152589379417)
XLA Ops:
  0.0 1.4 %copy.6.ids = s32[12,2]{1,0:T(8,128)} copy(s32[12,2]{0,1:T(2,128)} %param.3) | data formatting | bytes 192 | tf_op args[1]
  2.0 3.2 %slots.1 = bf16[2,4,14464]{2,1,0:T(4,128)(2,1)} custom-call(s32[2]{0:T(128)} %pad_add_fusion.where, s32[12,2]{1,0:T(8,128)} %copy.6.ids, bf16[12,14336]{1,0:T(8,128)(2,1)} %act.1), custom_call_target="tpu_custom_call" | custom-call | tf_op jit(solution)/shard_map/slots/pallas_call | solution.py:200
  7.9 4.0 %collective-permute-start.7 = (bf16[8,3584]{1,0:T(8,128)(2,1)S(1)}, bf16[8,3584]{1,0:T(8,128)(2,1)S(1)}, u32[]{:S(2)}, u32[]{:S(2)}) collective-permute-start(bf16[8,3584]{1,0:T(8,128)(2,1)S(1)} %pad_maximum_fusion.5), channel_id=1, source_target_pairs={{0,16},{1,17},{2,18},{3,19},{4,20},{5,21},{6,22},{7,23},{8,24},{9,... | collective-permute-start | bytes 172040 | tf_op jit(solution)/shard_map/ppermute | solution.py:187
  11.9 1.6 %collective-permute-start.11 = (bf16[8,3584]{1,0:T(8,128)(2,1)S(1)}, bf16[8,3584]{1,0:T(8,128)(2,1)S(1)}, u32[]{:S(2)}, u32[]{:S(2)}) collective-permute-start(bf16[8,3584]{1,0:T(8,128)(2,1)S(1)} %pad_maximum_fusion.5), channel_id=1, source_target_pairs={{0,8},{1,9},{2,10},{3,11},{4,12},{5,13},{6,14},{7,15},{8,0},{9,1},... | collective-permute-start | bytes 172040 | tf_op jit(solution)/shard_map/ppermute | solution.py:187
  14.2 1.6 %collective-permute-start.1 = (bf16[8,3712]{1,0:T(8,128)(2,1)S(1)}, bf16[8,3712]{1,0:T(8,128)(2,1)S(1)}, u32[]{:S(2)}, u32[]{:S(2)}) collective-permute-start(bf16[8,3712]{1,0:T(8,128)(2,1)S(1)} %get-tuple-element.20), channel_id=1, source_target_pairs={{0,8},{1,9},{2,10},{3,11},{4,12},{5,13},{6,14},{7,15},{8,0},{9,1},... | collective-permute-start | bytes 178184 | tf_op jit(solution)/shard_map/ppermute | solution.py:187
  16.2 1.8 %collective-permute-done.6 = bf16[8,3584]{1,0:T(8,128)(2,1)S(1)} collective-permute-done((bf16[8,3584]{1,0:T(8,128)(2,1)S(1)}, bf16[8,3584]{1,0:T(8,128)(2,1)S(1)}, u32[]{:S(2)}, u32[]{:S(2)}) %collective-permute-start.6) | collective-permute-done | bytes 57376 | tf_op jit(solution)/shard_map/ppermute | solution.py:187
  17.9 3.4 %collective-permute-start.3 = (bf16[8,3712]{1,0:T(8,128)(2,1)S(1)}, bf16[8,3712]{1,0:T(8,128)(2,1)S(1)}, u32[]{:S(2)}, u32[]{:S(2)}) collective-permute-start(bf16[8,3712]{1,0:T(8,128)(2,1)S(1)} %get-tuple-element.19), channel_id=1, source_target_pairs={{0,24},{1,25},{2,26},{3,27},{4,28},{5,29},{6,30},{7,31},{8,16},{9,... | collective-permute-start | bytes 178184 | tf_op jit(solution)/shard_map/ppermute | solution.py:187
  21.8 5.5 %collective-permute-done.8 = bf16[8,3584]{1,0:T(8,128)(2,1)S(1)} collective-permute-done((bf16[8,3584]{1,0:T(8,128)(2,1)S(1)}, bf16[8,3584]{1,0:T(8,128)(2,1)S(1)}, u32[]{:S(2)}, u32[]{:S(2)}) %collective-permute-start.8) | collective-permute-done | bytes 57376 | tf_op jit(solution)/shard_map/ppermute | solution.py:187
  28.4 4.0 %collective-permute-done.12 = bf16[8,3584]{1,0:T(8,128)(2,1)S(1)} collective-permute-done((bf16[8,3584]{1,0:T(8,128)(2,1)S(1)}, bf16[8,3584]{1,0:T(8,128)(2,1)S(1)}, u32[]{:S(2)}, u32[]{:S(2)}) %collective-permute-start.12) | collective-permute-done | bytes 57376 | tf_op jit(solution)/shard_map/ppermute | solution.py:187
  32.4 1.6 %collective-permute-done.13 = bf16[8,3584]{1,0:T(8,128)(2,1)S(1)} collective-permute-done((bf16[8,3584]{1,0:T(8,128)(2,1)S(1)}, bf16[8,3584]{1,0:T(8,128)(2,1)S(1)}, u32[]{:S(2)}, u32[]{:S(2)}) %collective-permute-start.13) | collective-permute-done | bytes 57376 | tf_op jit(solution)/shard_map/ppermute | solution.py:187
  34.0 1.3 %collective-permute-start.17 = (bf16[8,3584]{1,0:T(8,128)(2,1)S(1)}, bf16[8,3584]{1,0:T(8,128)(2,1)S(1)}, u32[]{:S(2)}, u32[]{:S(2)}) collective-permute-start(bf16[8,3584]{1,0:T(8,128)(2,1)S(1)} %pad_maximum_fusion.3), channel_id=1, source_target_pairs={{0,16},{1,17},{2,18},{3,19},{4,20},{5,21},{6,22},{7,23},{8,24},{9,... | collective-permute-start | bytes 172040 | tf_op jit(solution)/shard_map/ppermute | solution.py:187
  35.3 2.5 %concatenate.77 = bf16[32,3584]{1,0:T(8,128)(2,1)} concatenate(bf16[4,3584]{1,0:T(4,128)(2,1)S(1)} %get-tuple-element.12, bf16[4,3584]{1,0:T(4,128)(2,1)S(1)} %get-tuple-element.16, bf16[8,3584]{1,0:T(8,128)(2,1)S(1)} %collective-permute-done.11, bf16[8,3584]{1,0:T(8,128)(2,1)S(1)} %collective-permute-done.12, bf16[8,3584]{1,0:T(8,128)(2,1)S(1)} %collective-permute-done.13), dimensions={0} | concatenate | bytes 458752 | tf_op jit(solution)/shard_map/concatenate | solution.py:226
  37.8 2.4 %collective-permute-start.18 = (bf16[8,3584]{1,0:T(8,128)(2,1)S(1)}, bf16[8,3584]{1,0:T(8,128)(2,1)S(1)}, u32[]{:S(2)}, u32[]{:S(2)}) collective-permute-start(bf16[8,3584]{1,0:T(8,128)(2,1)S(1)} %pad_maximum_fusion.2), channel_id=1, source_target_pairs={{0,24},{1,25},{2,26},{3,27},{4,28},{5,29},{6,30},{7,31},{8,16},{9,... | collective-permute-start | bytes 172040 | tf_op jit(solution)/shard_map/ppermute | solution.py:187
  42.5 9.8 %collective-permute-done.4 = bf16[32,3712]{1,0:T(8,128)(2,1)S(1)} collective-permute-done((bf16[32,3712]{1,0:T(8,128)(2,1)S(1)}, bf16[32,3712]{1,0:T(8,128)(2,1)S(1)}, u32[]{:S(2)}, u32[]{:S(2)}) %collective-permute-start.4) | collective-permute-done | bytes 237600 | tf_op jit(solution)/shard_map/ppermute | solution.py:187
  52.6 2.6 %collective-permute-start.5 = (bf16[64,3712]{1,0:T(8,128)(2,1)S(1)}, bf16[64,3712]{1,0:T(8,128)(2,1)S(1)}, u32[]{:S(2)}, u32[]{:S(2)}) collective-permute-start(bf16[64,3712]{1,0:T(8,128)(2,1)S(1)} %constant_dynamic-update-slice_fusion.refs_0_.refs_2_), channel_id=1, source_target_pairs={{0,4},{1,3},{2,6},{3,1},{4,0},{5,7},{6,2},{7,5},{8,12},{9,11},{10,... | collective-permute-start | bytes 1425416 | tf_op jit(solution)/shard_map/ppermute | solution.py:187
  55.2 2.5 %concatenate.79 = bf16[32,3584]{1,0:T(8,128)(2,1)} concatenate(bf16[4,3584]{1,0:T(4,128)(2,1)S(1)} %get-tuple-element.11, bf16[4,3584]{1,0:T(4,128)(2,1)S(1)} %get-tuple-element.15, bf16[8,3584]{1,0:T(8,128)(2,1)S(1)} %collective-permute-done.16, bf16[8,3584]{1,0:T(8,128)(2,1)S(1)} %collective-permute-done.17, bf16[8,3584]{1,0:T(8,128)(2,1)S(1)} %collective-permute-done.18), dimensions={0} | concatenate | bytes 458752 | tf_op jit(solution)/shard_map/concatenate | solution.py:226
  59.2 1.8 %collective-permute-done.14 = bf16[32,3584]{1,0:T(8,128)(2,1)S(1)} collective-permute-done((bf16[32,3584]{1,0:T(8,128)(2,1)}, bf16[32,3584]{1,0:T(8,128)(2,1)S(1)}, u32[]{:S(2)}, u32[]{:S(2)}) %collective-permute-start.14) | collective-permute-done | bytes 229408 | tf_op jit(solution)/shard_map/ppermute | solution.py:187
  61.1 1.4 %collective-permute-start.15 = (bf16[64,3584]{1,0:T(8,128)(2,1)S(1)}, bf16[64,3584]{1,0:T(8,128)(2,1)S(1)}, u32[]{:S(2)}, u32[]{:S(2)}) collective-permute-start(bf16[64,3584]{1,0:T(8,128)(2,1)S(1)} %concatenate.78.refs_3_), channel_id=1, source_target_pairs={{0,4},{1,3},{2,6},{3,1},{4,0},{5,7},{6,2},{7,5},{8,12},{9,11},{10,... | collective-permute-start | bytes 1376264 | tf_op jit(solution)/shard_map/ppermute | solution.py:187
  62.5 4.0 %collective-permute-done.19 = bf16[32,3584]{1,0:T(8,128)(2,1)} collective-permute-done((bf16[32,3584]{1,0:T(8,128)(2,1)}, bf16[32,3584]{1,0:T(8,128)(2,1)}, u32[]{:S(2)}, u32[]{:S(2)}) %collective-permute-start.19) | collective-permute-done | bytes 229408 | tf_op jit(solution)/shard_map/ppermute | solution.py:187
  69.2 2.0 %left.1 = (bf16[896,128]{1,0:T(8,128)(2,1)}, f32[8,128]{1,0:T(8,128)}) custom-call(s32[1]{0:T(128)} %bitcast.4.where, bf16[64,3712]{1,0:T(8,128)(2,1)} %copy-done.2, bf16[64,3712]{1,0:T(8,128)(2,1)} %copy-done.4), custom_call_target="tpu_custom_call" | custom-call | flops 7340032 | bytes 458752 | tf_op jit(solution)/shard_map/left/pallas_call | solution.py:151
  74.9 5.1 %gram.4.refs_0_ = f32[1,896,14336]{2,1,0:T(8,128)} custom-call(s32[1]{0:T(128)} %bitcast.3.where, bf16[896,128]{1,0:T(8,128)(2,1)S(1)} %copy-done, f32[8,128]{1,0:T(8,128)S(1)} %copy-done.6, bf16[64,3712]{1,0:T(8,128)(2,1)S(1)} %copy-done.3, bf16[64,3712]{1,0:T(8,128)(2,1)S(1)} %copy-done.5), custom_call_target="tpu_custom_call" | custom-call | flops 822083584 | bytes 12845056 | tf_op jit(solution)/shard_map/gram/pallas_call | solution.py:110
  80.0 5.1 %gram.5.refs_0_ = f32[1,896,14336]{2,1,0:T(8,128)} custom-call(s32[1]{0:T(128)} %bitcast.2.where, f32[1,896,14336]{2,1,0:T(8,128)} %gram.4.refs_0_, bf16[896,128]{1,0:T(8,128)(2,1)S(1)} %copy-done.1, f32[8,128]{1,0:T(8,128)S(1)} %copy-done.6, bf16[64,3584]{1,0:T(8,128)(2,1)S(1)} %concatenate.76.refs_3_, ...), custom_call_target="tpu_custom_call", output_to_operand_aliasing={{}: (1, {})} | custom-call | flops 822083584 | bytes 12845056 | tf_op jit(solution)/shard_map/gram/pallas_call | solution.py:110
  85.2 5.2 %gram.6.refs_0_ = f32[1,896,14336]{2,1,0:T(8,128)} custom-call(s32[1]{0:T(128)} %bitcast.1.where, f32[1,896,14336]{2,1,0:T(8,128)} %gram.5.refs_0_, bf16[896,128]{1,0:T(8,128)(2,1)S(1)} %copy-done.1, f32[8,128]{1,0:T(8,128)S(1)} %copy-done.6, bf16[64,3584]{1,0:T(8,128)(2,1)S(1)} %concatenate.78.refs_3_, ...), custom_call_target="tpu_custom_call", output_to_operand_aliasing={{}: (1, {})} | custom-call | flops 822083584 | bytes 12845056 | tf_op jit(solution)/shard_map/gram/pallas_call | solution.py:110
  90.4 6.2 %gram.7 = f32[1,896,14336]{2,1,0:T(8,128)} custom-call(s32[1]{0:T(128)} %bitcast.where, f32[1,896,14336]{2,1,0:T(8,128)} %gram.6.refs_0_, bf16[896,128]{1,0:T(8,128)(2,1)S(1)} %copy-done.1, f32[8,128]{1,0:T(8,128)S(1)} %copy-done.6, bf16[64,3584]{1,0:T(8,128)(2,1)S(1)} %concatenate.80.refs_3_, ...), custom_call_target="tpu_custom_call", output_to_operand_aliasing={{}: (1, {})} | custom-call | flops 822083584 | bytes 12845056 | tf_op jit(solution)/shard_map/gram/pallas_call | solution.py:110
  (61 shorter events, 16.3 us)
Async XLA Ops:
  6.3 1.5 %collective-permute-start = (bf16[4,14464]{1,0:T(4,128)(2,1)S(1)}, bf16[4,14464]{1,0:T(4,128)(2,1)S(1)}, u32[]{:S(2)}, u32[]{:S(2)}) collective-permute-start(bf16[4,14464]{1,0:T(4,128)(2,1)S(1)} %get-tuple-element.10), channel_id=1, source_target_pairs={{0,1},{1,0},{2,3},{3,2},{4,5},{5,4},{6,7},{7,6},{8,9},{9,8},{10,11... | collective-permute-start | bytes 347144 | tf_op jit(solution)/shard_map/ppermute | solution.py:213
  7.9 13.4 %collective-permute-start.7 = (bf16[8,3584]{1,0:T(8,128)(2,1)S(1)}, bf16[8,3584]{1,0:T(8,128)(2,1)S(1)}, u32[]{:S(2)}, u32[]{:S(2)}) collective-permute-start(bf16[8,3584]{1,0:T(8,128)(2,1)S(1)} %pad_maximum_fusion.5), channel_id=1, source_target_pairs={{0,16},{1,17},{2,18},{3,19},{4,20},{5,21},{6,22},{7,23},{8,24},{9,... | collective-permute-start | bytes 172040 | tf_op jit(solution)/shard_map/ppermute | solution.py:187
  11.9 15.4 %collective-permute-start.11 = (bf16[8,3584]{1,0:T(8,128)(2,1)S(1)}, bf16[8,3584]{1,0:T(8,128)(2,1)S(1)}, u32[]{:S(2)}, u32[]{:S(2)}) collective-permute-start(bf16[8,3584]{1,0:T(8,128)(2,1)S(1)} %pad_maximum_fusion.5), channel_id=1, source_target_pairs={{0,8},{1,9},{2,10},{3,11},{4,12},{5,13},{6,14},{7,15},{8,0},{9,1},... | collective-permute-start | bytes 172040 | tf_op jit(solution)/shard_map/ppermute | solution.py:187
  13.5 4.4 %collective-permute-start.6 = (bf16[8,3584]{1,0:T(8,128)(2,1)S(1)}, bf16[8,3584]{1,0:T(8,128)(2,1)S(1)}, u32[]{:S(2)}, u32[]{:S(2)}) collective-permute-start(bf16[8,3584]{1,0:T(8,128)(2,1)S(1)} %pad_maximum_fusion.2), channel_id=1, source_target_pairs={{0,8},{1,9},{2,10},{3,11},{4,12},{5,13},{6,14},{7,15},{8,0},{9,1},... | collective-permute-start | bytes 172040 | tf_op jit(solution)/shard_map/ppermute | solution.py:187
  14.2 23.6 %collective-permute-start.1 = (bf16[8,3712]{1,0:T(8,128)(2,1)S(1)}, bf16[8,3712]{1,0:T(8,128)(2,1)S(1)}, u32[]{:S(2)}, u32[]{:S(2)}) collective-permute-start(bf16[8,3712]{1,0:T(8,128)(2,1)S(1)} %get-tuple-element.20), channel_id=1, source_target_pairs={{0,8},{1,9},{2,10},{3,11},{4,12},{5,13},{6,14},{7,15},{8,0},{9,1},... | collective-permute-start | bytes 178184 | tf_op jit(solution)/shard_map/ppermute | solution.py:187
  15.8 24.4 %collective-permute-start.2 = (bf16[8,3712]{1,0:T(8,128)(2,1)S(1)}, bf16[8,3712]{1,0:T(8,128)(2,1)S(1)}, u32[]{:S(2)}, u32[]{:S(2)}) collective-permute-start(bf16[8,3712]{1,0:T(8,128)(2,1)S(1)} %get-tuple-element.21), channel_id=1, source_target_pairs={{0,16},{1,17},{2,18},{3,19},{4,20},{5,21},{6,22},{7,23},{8,24},{9,... | collective-permute-start | bytes 178184 | tf_op jit(solution)/shard_map/ppermute | solution.py:187
  17.9 23.3 %collective-permute-start.3 = (bf16[8,3712]{1,0:T(8,128)(2,1)S(1)}, bf16[8,3712]{1,0:T(8,128)(2,1)S(1)}, u32[]{:S(2)}, u32[]{:S(2)}) collective-permute-start(bf16[8,3712]{1,0:T(8,128)(2,1)S(1)} %get-tuple-element.19), channel_id=1, source_target_pairs={{0,24},{1,25},{2,26},{3,27},{4,28},{5,29},{6,30},{7,31},{8,16},{9,... | collective-permute-start | bytes 178184 | tf_op jit(solution)/shard_map/ppermute | solution.py:187
  21.3 6.0 %collective-permute-start.8 = (bf16[8,3584]{1,0:T(8,128)(2,1)S(1)}, bf16[8,3584]{1,0:T(8,128)(2,1)S(1)}, u32[]{:S(2)}, u32[]{:S(2)}) collective-permute-start(bf16[8,3584]{1,0:T(8,128)(2,1)S(1)} %pad_maximum_fusion.4), channel_id=1, source_target_pairs={{0,24},{1,25},{2,26},{3,27},{4,28},{5,29},{6,30},{7,31},{8,16},{9,... | collective-permute-start | bytes 172040 | tf_op jit(solution)/shard_map/ppermute | solution.py:187
  27.3 5.1 %collective-permute-start.12 = (bf16[8,3584]{1,0:T(8,128)(2,1)S(1)}, bf16[8,3584]{1,0:T(8,128)(2,1)S(1)}, u32[]{:S(2)}, u32[]{:S(2)}) collective-permute-start(bf16[8,3584]{1,0:T(8,128)(2,1)S(1)} %pad_maximum_fusion.2), channel_id=1, source_target_pairs={{0,16},{1,17},{2,18},{3,19},{4,20},{5,21},{6,22},{7,23},{8,24},{9,... | collective-permute-start | bytes 172040 | tf_op jit(solution)/shard_map/ppermute | solution.py:187
  27.3 6.7 %collective-permute-start.13 = (bf16[8,3584]{1,0:T(8,128)(2,1)S(1)}, bf16[8,3584]{1,0:T(8,128)(2,1)S(1)}, u32[]{:S(2)}, u32[]{:S(2)}) collective-permute-start(bf16[8,3584]{1,0:T(8,128)(2,1)S(1)} %pad_maximum_fusion.3), channel_id=1, source_target_pairs={{0,24},{1,25},{2,26},{3,27},{4,28},{5,29},{6,30},{7,31},{8,16},{9,... | collective-permute-start | bytes 172040 | tf_op jit(solution)/shard_map/ppermute | solution.py:187
  32.4 20.2 %collective-permute-start.16 = (bf16[8,3584]{1,0:T(8,128)(2,1)S(1)}, bf16[8,3584]{1,0:T(8,128)(2,1)S(1)}, u32[]{:S(2)}, u32[]{:S(2)}) collective-permute-start(bf16[8,3584]{1,0:T(8,128)(2,1)S(1)} %pad_maximum_fusion.4), channel_id=1, source_target_pairs={{0,8},{1,9},{2,10},{3,11},{4,12},{5,13},{6,14},{7,15},{8,0},{9,1},... | collective-permute-start | bytes 172040 | tf_op jit(solution)/shard_map/ppermute | solution.py:187
  34.0 21.3 %collective-permute-start.17 = (bf16[8,3584]{1,0:T(8,128)(2,1)S(1)}, bf16[8,3584]{1,0:T(8,128)(2,1)S(1)}, u32[]{:S(2)}, u32[]{:S(2)}) collective-permute-start(bf16[8,3584]{1,0:T(8,128)(2,1)S(1)} %pad_maximum_fusion.3), channel_id=1, source_target_pairs={{0,16},{1,17},{2,18},{3,19},{4,20},{5,21},{6,22},{7,23},{8,24},{9,... | collective-permute-start | bytes 172040 | tf_op jit(solution)/shard_map/ppermute | solution.py:187
  37.8 17.4 %collective-permute-start.18 = (bf16[8,3584]{1,0:T(8,128)(2,1)S(1)}, bf16[8,3584]{1,0:T(8,128)(2,1)S(1)}, u32[]{:S(2)}, u32[]{:S(2)}) collective-permute-start(bf16[8,3584]{1,0:T(8,128)(2,1)S(1)} %pad_maximum_fusion.2), channel_id=1, source_target_pairs={{0,24},{1,25},{2,26},{3,27},{4,28},{5,29},{6,30},{7,31},{8,16},{9,... | collective-permute-start | bytes 172040 | tf_op jit(solution)/shard_map/ppermute | solution.py:187
  40.3 18.0 %collective-permute-start.9 = (bf16[32,3584]{1,0:T(8,128)(2,1)S(1)}, bf16[32,3584]{1,0:T(8,128)(2,1)S(1)}, u32[]{:S(2)}, u32[]{:S(2)}) collective-permute-start(bf16[32,3584]{1,0:T(8,128)(2,1)S(1)} %concatenate.75), channel_id=1, source_target_pairs={{0,2},{1,5},{2,0},{3,7},{4,6},{5,1},{6,4},{7,3},{8,10},{9,13},{10,... | collective-permute-start | bytes 688136 | tf_op jit(solution)/shard_map/ppermute | solution.py:187
  41.2 11.0 %collective-permute-start.4 = (bf16[32,3712]{1,0:T(8,128)(2,1)S(1)}, bf16[32,3712]{1,0:T(8,128)(2,1)S(1)}, u32[]{:S(2)}, u32[]{:S(2)}) collective-permute-start(bf16[32,3712]{1,0:T(8,128)(2,1)S(1)} %pad_maximum_fusion), channel_id=1, source_target_pairs={{0,2},{1,5},{2,0},{3,7},{4,6},{5,1},{6,4},{7,3},{8,10},{9,13},{10,... | collective-permute-start | bytes 712712 | tf_op jit(solution)/shard_map/ppermute | solution.py:187
  52.3 8.7 %collective-permute-start.14 = (bf16[32,3584]{1,0:T(8,128)(2,1)}, bf16[32,3584]{1,0:T(8,128)(2,1)S(1)}, u32[]{:S(2)}, u32[]{:S(2)}) collective-permute-start(bf16[32,3584]{1,0:T(8,128)(2,1)} %concatenate.77), channel_id=1, source_target_pairs={{0,2},{1,5},{2,0},{3,7},{4,6},{5,1},{6,4},{7,3},{8,10},{9,13},{10,... | collective-permute-start | bytes 688136 | tf_op jit(solution)/shard_map/ppermute | solution.py:187
  52.6 15.8 %copy-start.2 = (bf16[64,3712]{1,0:T(8,128)(2,1)}, bf16[64,3712]{1,0:T(8,128)(2,1)S(1)}, u32[]{:S(2)}) copy-start(bf16[64,3712]{1,0:T(8,128)(2,1)S(1)} %constant_dynamic-update-slice_fusion.refs_0_.refs_2_) | copy-start | bytes 1425412
  52.6 15.8 %collective-permute-start.5 = (bf16[64,3712]{1,0:T(8,128)(2,1)S(1)}, bf16[64,3712]{1,0:T(8,128)(2,1)S(1)}, u32[]{:S(2)}, u32[]{:S(2)}) collective-permute-start(bf16[64,3712]{1,0:T(8,128)(2,1)S(1)} %constant_dynamic-update-slice_fusion.refs_0_.refs_2_), channel_id=1, source_target_pairs={{0,4},{1,3},{2,6},{3,1},{4,0},{5,7},{6,2},{7,5},{8,12},{9,11},{10,... | collective-permute-start | bytes 1425416 | tf_op jit(solution)/shard_map/ppermute | solution.py:187
  57.8 8.8 %collective-permute-start.19 = (bf16[32,3584]{1,0:T(8,128)(2,1)}, bf16[32,3584]{1,0:T(8,128)(2,1)}, u32[]{:S(2)}, u32[]{:S(2)}) collective-permute-start(bf16[32,3584]{1,0:T(8,128)(2,1)} %concatenate.79), channel_id=1, source_target_pairs={{0,2},{1,5},{2,0},{3,7},{4,6},{5,1},{6,4},{7,3},{8,10},{9,13},{10,... | collective-permute-start | bytes 688136 | tf_op jit(solution)/shard_map/ppermute | solution.py:187
  58.5 21.6 %collective-permute-start.10 = (bf16[64,3584]{1,0:T(8,128)(2,1)S(1)}, bf16[64,3584]{1,0:T(8,128)(2,1)S(1)}, u32[]{:S(2)}, u32[]{:S(2)}) collective-permute-start(bf16[64,3584]{1,0:T(8,128)(2,1)S(1)} %concatenate.76.refs_3_), channel_id=1, source_target_pairs={{0,4},{1,3},{2,6},{3,1},{4,0},{5,7},{6,2},{7,5},{8,12},{9,11},{10,... | collective-permute-start | bytes 1376264 | tf_op jit(solution)/shard_map/ppermute | solution.py:187
  61.1 24.1 %collective-permute-start.15 = (bf16[64,3584]{1,0:T(8,128)(2,1)S(1)}, bf16[64,3584]{1,0:T(8,128)(2,1)S(1)}, u32[]{:S(2)}, u32[]{:S(2)}) collective-permute-start(bf16[64,3584]{1,0:T(8,128)(2,1)S(1)} %concatenate.78.refs_3_), channel_id=1, source_target_pairs={{0,4},{1,3},{2,6},{3,1},{4,0},{5,7},{6,2},{7,5},{8,12},{9,11},{10,... | collective-permute-start | bytes 1376264 | tf_op jit(solution)/shard_map/ppermute | solution.py:187
  67.6 22.8 %collective-permute-start.20 = (bf16[64,3584]{1,0:T(8,128)(2,1)S(1)}, bf16[64,3584]{1,0:T(8,128)(2,1)}, u32[]{:S(2)}, u32[]{:S(2)}) collective-permute-start(bf16[64,3584]{1,0:T(8,128)(2,1)S(1)} %concatenate.80.refs_3_), channel_id=1, source_target_pairs={{0,4},{1,3},{2,6},{3,1},{4,0},{5,7},{6,2},{7,5},{8,12},{9,11},{10,... | collective-permute-start | bytes 1376264 | tf_op jit(solution)/shard_map/ppermute | solution.py:187
  73.2 1.0 %copy-start.5 = (bf16[64,3712]{1,0:T(8,128)(2,1)S(1)}, bf16[64,3712]{1,0:T(8,128)(2,1)}, u32[]{:S(2)}) copy-start(bf16[64,3712]{1,0:T(8,128)(2,1)} %copy-done.4) | copy-start | bytes 1425412
  74.9 5.2 %copy-start.1 = (bf16[896,128]{1,0:T(8,128)(2,1)S(1)}, bf16[896,128]{1,0:T(8,128)(2,1)}, u32[]{:S(2)}) copy-start(bf16[896,128]{1,0:T(8,128)(2,1)} %get-tuple-element.7.refs_0_.refs_1_) | copy-start | bytes 688132
  (4 other events, 3.4 us)
